TPU v7x, 32 devices: a whole 2x2x4 slice. The times are simulated.
32 devices in a mesh: row: 4 (over y, x), col: 8 (over z, core).
Axes of the slice: x: 2, y: 2, z: 4, core: 2. Of those that a mesh axis runs over, the one named last changes fastest.
Arguments:
- amplitudes: bfloat16 [800, 800, 768], P('row', 'col'), may hold values from -6 to 6
- integrals: bfloat16 [800, 800, 256], P('row', 'col'), may hold values from -0.375 to 0.375
- window_index: int32 [256], replicated, may hold values from 0 to 639999, as said below
Outputs:
- residual: bfloat16 [800, 800, 768], P('row', 'col')
- pair_energy: float32 [768], replicated
Inputs may be any that keep to these rules, and one draw needn't show every extreme that they name: `window_index`: the window pairs are distinct; pair k lies in the block of a rows and b columns owned by device number k // 8 in row-major order of the (a, b) device grid, 8 pairs for each block.
All inputs are finite; a program needn't handle non-finite values.
Results may differ from a plain program's by a relative error of at most 0.001.
Values may be sent and summed in bfloat16 or wider, within the bound.
A program may use at most 256 MiB of HBM per device.

v0:
```python
import jax
import jax.numpy as jnp
from jax import lax
from jax.sharding import PartitionSpec as P


def shards(amplitudes, integrals, window_index):
    block_rows, block_cols, pairs = amplitudes.shape
    window = integrals.shape[2]
    ncols = lax.axis_size("col")
    nrows = lax.axis_size("row")
    per_device = window // (nrows * ncols)
    row_rank = lax.axis_index("row")
    col_rank = lax.axis_index("col")
    linear_rank = row_rank * ncols + col_rank
    owned_index = lax.dynamic_slice_in_dim(window_index, linear_rank * per_device, per_device)
    virtuals = block_rows * nrows
    row_offset = owned_index // virtuals - row_rank * block_rows
    col_offset = owned_index % virtuals - col_rank * block_cols
    owned = amplitudes[row_offset, col_offset]
    in_row = lax.all_gather(owned, "col", axis=0, tiled=True)
    columns = lax.all_gather(in_row, "row", axis=0, tiled=True)
    full = jnp.einsum("abk,kp->abp", integrals, columns, preferred_element_type=jnp.float32)
    partial_value = jnp.sum(amplitudes.astype(jnp.float32) * full, axis=(0, 1))
    pair_energy = lax.psum(partial_value, ("row", "col")) / virtuals
    residual = full.astype(jnp.bfloat16)
    return (residual, pair_energy)


def solution(mesh):
    return jax.shard_map(
        shards,
        mesh=mesh,
        in_specs=(P("row", "col", None), P("row", "col", None), P()),
        out_specs=(P("row", "col", None), P()),
        check_vma=False,
    )
```

profile of v0, /device:TPU:0, one launch (start us, length us, event | category | flops | bytes accessed | tf_op | source)
XLA Modules:
  0.0 172.8 jit_solution(1093921430304254708)
XLA Ops:
  0.6 0.8 fusion.7
  1.4 1.4 gather_fusion
  2.8 15.6 %all_gather.6 = bf16[64,768]{1,0:T(8,128)(2,1)S(1)} all-gather(bf16[8,768]{1,0:T(8,128)(2,1)S(1)} %gather_fusion), channel_id=1, replica_groups=mesh['row'=4,'col'=8] {'col'}, dimensions={0}, use_global_device_ids=true | all-gather | bytes 110592 | tf_op jit(solution)/shard_map/all_gather | solution.py:21
  18.4 9.5 %all_gather.7 = bf16[256,768]{1,0:T(8,128)(2,1)S(1)} all-gather(bf16[64,768]{1,0:T(8,128)(2,1)S(1)} %all_gather.6), channel_id=1, replica_groups=mesh['row'=4,'col'=8] {'row'}, dimensions={0}, use_global_device_ids=true | all-gather | bytes 491520 | tf_op jit(solution)/shard_map/all_gather | solution.py:22
  27.9 44.0 %bitcast_convert_fusion = (bf16[200,100,768]{2,1,0:T(8,128)(2,1)}, f32[768,200,100]{0,2,1:T(8,128)}) fusion(bf16[200,100,256]{2,0,1:T(8,128)(2,1)} %param.4, bf16[256,768]{1,0:T(8,128)(2,1)S(1)} %all_gather.7), kind=kOutput, calls=%fused_computation.2 | convolution fusion | flops 7879680000 | bytes 102793216 | tf_op jit(solution)/shard_map/abk,kp->abp/dot_general | solution.py:23
  71.9 22.0 %copy.7 = bf16[200,100,768]{2,0,1:T(8,128)(2,1)} copy(bf16[200,100,768]{2,1,0:T(8,128)(2,1)} %get-tuple-element.4) | data formatting | bytes 61440000
  93.9 39.0 %fusion = f32[768]{0:T(1024)S(1)} fusion(f32[768,200,100]{0,2,1:T(8,128)} %get-tuple-element.5, bf16[200,100,768]{2,0,1:T(8,128)(2,1)} %param.3), kind=kLoop, calls=%fused_computation.3 | loop fusion | flops 46079232 | bytes 92163072 | tf_op jit(solution)/shard_map/reduce_sum | solution.py:24
  132.9 39.3 %psum.7 = f32[768]{0:T(1024)S(1)} all-reduce(f32[768]{0:T(1024)S(1)} %fusion), channel_id=1, replica_groups=mesh['row'=4,'col'=8] {'row','col'}, use_global_device_ids=true, to_apply=%region_1.2 | all-reduce | flops 768 | bytes 6144 | tf_op jit(solution)/shard_map/psum | solution.py:25
  172.2 0.6 broadcast_multiply_fusion
where the time goes:
time: 173 us
  blocking collectives  64.5 us (37%)
  matrix products  44 us (25%)
  other arithmetic  40.3 us (23%)
  local copies, waits for them, and re-layouts  23.3 us (13%)
    dot_general x1, matrix products, shards(): jnp.einsum('abk,kp->abp', integrals, columns, preferred_element_type=jnp....  44 us
    psum x1, blocking collectives, shards(): pair_energy = lax.psum(partial_value, ('row', 'col')) / virtuals  39.3 us
    reduce_sum x1, other arithmetic, shards(): partial_value = jnp.sum(amplitudes.astype(jnp.float32) * full, axis=(0, 1))  39 us
    unnamed x1, local copies, waits for them, and re-layouts  22 us
    all_gather x1, blocking collectives, shards(): in_row = lax.all_gather(owned, 'col', axis=0, tiled=True)  15.6 us
    all_gather x1, blocking collectives, shards(): columns = lax.all_gather(in_row, 'row', axis=0, tiled=True)  9.5 us

commit v1 on v0

--- a/solution.py
+++ b/solution.py
@@ -1,7 +1,132 @@
+import functools
+
 import jax
 import jax.numpy as jnp
 from jax import lax
+from jax.experimental import pallas as pl
+from jax.experimental.pallas import tpu as pltpu
 from jax.sharding import PartitionSpec as P
+
+MESH = pl.DeviceIdType.MESH
+
+
+def exchange_kernel(nrows, ncols, own_ref, out_ref, send_sems, recv_sems):
+    count = nrows * ncols
+    me = lax.axis_index("row") * ncols + lax.axis_index("col")
+
+    def place(step):
+        other = lax.rem(me + step, count)
+        return (other // ncols, lax.rem(other, ncols))
+
+    barrier = pltpu.get_barrier_semaphore()
+
+    def greet(step, carry):
+        pl.semaphore_signal(barrier, inc=1, device_id=place(step), device_id_type=MESH)
+        return carry
+
+    lax.fori_loop(1, count, greet, 0)
+    pl.semaphore_wait(barrier, count - 1)
+
+    def copy(step, slot):
+        return pltpu.make_async_remote_copy(
+            src_ref=own_ref,
+            dst_ref=out_ref.at[slot],
+            send_sem=send_sems.at[step],
+            recv_sem=recv_sems.at[step],
+            device_id=place(step),
+            device_id_type=MESH,
+        )
+
+    def send(step, carry):
+        copy(step, me).start()
+        return carry
+
+    lax.fori_loop(1, count, send, 0)
+    out_ref[me] = own_ref[...]
+
+    def finish(step, carry):
+        source = lax.rem(me + count - step, count)
+        copy(step, source).wait_recv()
+        copy(step, me).wait_send()
+        return carry
+
+    lax.fori_loop(1, count, finish, 0)
+
+
+def exchange(block, nrows, ncols, collective_id):
+    count = nrows * ncols
+    return pl.pallas_call(
+        functools.partial(exchange_kernel, nrows, ncols),
+        out_shape=jax.ShapeDtypeStruct((count,) + block.shape, block.dtype),
+        in_specs=[pl.BlockSpec(memory_space=pltpu.VMEM)],
+        out_specs=pl.BlockSpec(memory_space=pltpu.VMEM),
+        scratch_shapes=[
+            pltpu.SemaphoreType.DMA((count,)),
+            pltpu.SemaphoreType.DMA((count,)),
+        ],
+        compiler_params=pltpu.CompilerParams(collective_id=collective_id, has_side_effects=True),
+    )(block)
+
+
+ROWS = 2000
+SUB = 200
+
+
+def largest_divisor(extent, most, multiple):
+    fits = [d for d in range(multiple, min(extent, most) + 1, multiple) if extent % d == 0]
+    return max(fits) if fits else extent
+
+
+def ladder_kernel(sub, chunk, amps_ref, ints_ref, cols_ref, residual_ref, energy_ref, total_ref):
+    rows, pairs = amps_ref.shape
+
+    @pl.when(pl.program_id(0) == 0)
+    def _():
+        total_ref[...] = jnp.zeros_like(total_ref)
+
+    for start in range(0, pairs, chunk):
+        span = slice(start, start + chunk)
+        total = jnp.zeros((8, chunk), jnp.float32)
+        for low in range(0, rows, sub):
+            part = slice(low, low + sub)
+            full = jnp.dot(ints_ref[part], cols_ref[:, span], preferred_element_type=jnp.float32)
+            residual_ref[part, span] = full.astype(residual_ref.dtype)
+            weighted = amps_ref[part, span].astype(jnp.float32) * full
+            total = total + jnp.sum(weighted.reshape(sub // 8, 8, chunk), axis=0)
+        total_ref[:, span] += total
+
+    @pl.when(pl.program_id(0) == pl.num_programs(0) - 1)
+    def _():
+        energy_ref[...] = jnp.sum(total_ref[...], axis=0, keepdims=True)
+
+
+def ladder(amplitudes, integrals, columns):
+    cells, pairs = amplitudes.shape
+    window = integrals.shape[1]
+    rows = largest_divisor(cells, ROWS, 8)
+    sub = largest_divisor(rows, SUB, 8)
+    chunk = 256 if pairs % 256 == 0 else pairs
+    return pl.pallas_call(
+        functools.partial(ladder_kernel, sub, chunk),
+        grid=(cells // rows,),
+        out_shape=(
+            jax.ShapeDtypeStruct((cells, pairs), jnp.bfloat16),
+            jax.ShapeDtypeStruct((1, pairs), jnp.float32),
+        ),
+        in_specs=[
+            pl.BlockSpec((rows, pairs), lambda i: (i, 0)),
+            pl.BlockSpec((rows, window), lambda i: (i, 0)),
+            pl.BlockSpec((window, pairs), lambda i: (0, 0)),
+        ],
+        out_specs=(
+            pl.BlockSpec((rows, pairs), lambda i: (i, 0)),
+            pl.BlockSpec((1, pairs), lambda i: (0, 0)),
+        ),
+        scratch_shapes=[pltpu.VMEM((8, pairs), jnp.float32)],
+        compiler_params=pltpu.CompilerParams(
+            dimension_semantics=("arbitrary",), vmem_limit_bytes=60 * 1024 * 1024
+        ),
+    )(amplitudes, integrals, columns)
 
 
 def shards(amplitudes, integrals, window_index):
@@ -18,12 +143,16 @@
     row_offset = owned_index // virtuals - row_rank * block_rows
     col_offset = owned_index % virtuals - col_rank * block_cols
     owned = amplitudes[row_offset, col_offset]
-    in_row = lax.all_gather(owned, "col", axis=0, tiled=True)
-    columns = lax.all_gather(in_row, "row", axis=0, tiled=True)
-    full = jnp.einsum("abk,kp->abp", integrals, columns, preferred_element_type=jnp.float32)
-    partial_value = jnp.sum(amplitudes.astype(jnp.float32) * full, axis=(0, 1))
-    pair_energy = lax.psum(partial_value, ("row", "col")) / virtuals
-    residual = full.astype(jnp.bfloat16)
+    columns = exchange(owned, nrows, ncols, 0).reshape(window, pairs)
+    cells = block_rows * block_cols
+    residual, partial_value = ladder(
+        amplitudes.transpose(1, 0, 2).reshape(cells, pairs),
+        integrals.transpose(1, 0, 2).reshape(cells, window),
+        columns,
+    )
+    residual = residual.reshape(block_cols, block_rows, pairs).transpose(1, 0, 2)
+    values = exchange(partial_value, nrows, ncols, 1)
+    pair_energy = jnp.sum(values[:, 0, :], axis=0) / virtuals
     return (residual, pair_energy)
 
 

time: 173 us -> 61.4 us (0.35)
  blocking collectives: 64.5 us -> 0 us
  Pallas kernels: 0 us -> 56.1 us
  matrix products: 44 us -> 0 us
  other arithmetic: 40.3 us -> 2.34 us
  local copies, waits for them, and re-layouts: 23.3 us -> 1.97 us
    pallas_call x0 -> x3, Pallas kernels: none -> 56.1 us  [the longest x2 28.4 us: exchange(): pl.pallas_call(functools.partial(exchange_kernel, nrows, ncols), out_shap...]
    dot_general x1 -> x0, matrix products: 44 us -> none  [shards(): jnp.einsum('abk,kp->abp', integrals, columns, preferred_element_type=jnp....]
    psum x1 -> x0, blocking collectives: 39.3 us -> none  [shards(): pair_energy = lax.psum(partial_value, ('row', 'col')) / virtuals]
    reduce_sum x1, other arithmetic: 39 us -> 0.97 us  [shards(): pair_energy = jnp.sum(values[:, 0, :], axis=0) / virtuals]
    all_gather x2 -> x0, blocking collectives: 25.1 us -> none  [the longest x1 15.6 us: shards(): in_row = lax.all_gather(owned, 'col', axis=0, tiled=True)]
    unnamed x1 -> x0, local copies, waits for them, and re-layouts: 22 us -> none
where the time goes in v1:
time: 61.4 us; the launch traced here: 61.1 us
  Pallas kernels  56.1 us (91%)
  other arithmetic  2.34 us (4%)
  local copies, waits for them, and re-layouts  1.97 us (3%)
  between operations  0.65 us (1%)
    pallas_call x2, Pallas kernels, exchange(): pl.pallas_call(functools.partial(exchange_kernel, nrows, ncols), out_shap...  28.4 us
    pallas_call x1, Pallas kernels, ladder(): pl.pallas_call(functools.partial(ladder_kernel, sub, chunk), grid=(cells...  27.8 us
    gather x1, local copies, waits for them, and re-layouts, shards(): owned = amplitudes[row_offset, col_offset]  1.97 us

profile of v1, /device:TPU:0, one launch (start us, length us, event | category | flops | bytes accessed | tf_op | source)
XLA Modules:
  0.0 61.1 jit_solution(17818447023833055575)
XLA Ops:
  0.6 0.8 %fusion.3 = s32[8]{0:T(128)S(1)} fusion(s32[256]{0:T(256)} %param.5, s32[]{:T(128)S(6)} %select_n.21, s32[]{:T(128)S(6)} %mul.15, s32[]{:T(128)S(6)} %mul.14), kind=kLoop, calls=%fused_computation.9 | loop fusion | flops 200 | bytes 76 | tf_op jit(solution)/shard_map/concatenate | solution.py:145
  1.4 2.0 %gather_fusion = bf16[8,768]{1,0:T(8,128)(2,1)} fusion(bf16[200,100,768]{2,0,1:T(8,128)(2,1)} %param.3, s32[8]{0:T(128)S(1)} %fusion.3), kind=kCustom, calls=%fused_computation | custom fusion | bytes 24640 | tf_op jit(solution)/shard_map/gather | solution.py:145
  3.4 18.2 %shard_map.50 = bf16[32,8,768]{2,1,0:T(8,128)(2,1)} custom-call(bf16[8,768]{1,0:T(8,128)(2,1)} %gather_fusion), custom_call_target="tpu_custom_call" | custom-call | tf_op jit(solution)/shard_map/pallas_call | solution.py:58
  21.6 27.8 %shard_map.51 = (bf16[20000,768]{1,0:T(8,128)(2,1)}, f32[1,768]{1,0:T(1,128)}) custom-call(bf16[20000,768]{1,0:T(8,128)(2,1)} %bitcast.10, bf16[20000,256]{1,0:T(8,128)(2,1)} %bitcast.11, bf16[256,768]{1,0:T(8,128)(2,1)} %bitcast.12), custom_call_target="tpu_custom_call" | custom-call | tf_op jit(solution)/shard_map/pallas_call | solution.py:109
  49.3 10.2 %shard_map.52 = f32[32,1,768]{2,1,0:T(1,128)} custom-call(f32[1,768]{1,0:T(1,128)} %get-tuple-element.5.own_ref), custom_call_target="tpu_custom_call" | custom-call | tf_op jit(solution)/shard_map/pallas_call | solution.py:58
  59.5 1.0 %reduce_sum.9 = f32[768]{0:T(1024)S(1)} reduce(f32[32,1,768]{2,1,0:T(1,128)} %shard_map.52, f32[]{:T(128)} %constant.43.clone.1), dimensions={0,1}, to_apply=%region_0.1 | reduce | flops 23808 | bytes 101380 | tf_op jit(solution)/shard_map/reduce_sum | solution.py:155
  60.5 0.6 broadcast_multiply_fusion
